TPU v7x, 512 devices: a whole 4x8x8 slice. The times are simulated.
512 devices in a mesh: grp: 16 (over y, core), mem: 32 (over x, z).
Axes of the slice: x: 4, y: 8, z: 8, core: 2. Of those that a mesh axis runs over, the one named last changes fastest.
Arguments:
- v_stack: bfloat16 [524288, 512], P(('grp', 'mem')), may hold values from -0.1875 to 0.1875
- u_stack: bfloat16 [524288, 512], P(('grp', 'mem')), may hold values from -0.25 to 0.25
- warm_start: bfloat16 [524288, 256], P(('grp', 'mem')), may hold values from -3 to 3
- observed: bfloat16 [524288, 256], P(('grp', 'mem')), may hold values from -12 to 12, as said below
- owners: int32 [512, 4], replicated, may hold values from 0 to 511, as said below
- tile_ranks: int32 [512, 4], P(('grp', 'mem')), may hold values from 8 to 128
Outputs:
- model: float32 [524288, 256], P(('grp', 'mem'))
- residual: bfloat16 [524288, 256], P(('grp', 'mem'))
Inputs may be any that keep to these rules, and one draw needn't show every extreme that they name: Writing d = g * 32 + m, owners[d, t] = ((g + a_t) mod 16) * 32 + (m + b_t) mod 32, where the offsets a_t differ over t, the offsets b_t differ over t, some slot has a_t = 15, some slot has a_t = 8, some slot has b_t = 31 and some slot has b_t = 16. `observed`: entries of one row block share a scale.
All inputs are finite; a program needn't handle non-finite values.
Results may differ from a plain program's by a relative error of at most 0.006.
Values may be sent and summed in bfloat16 or wider, within the bound.
No kernel may reach another device: no remote copies, remote signals or barrier semaphores. Data moves between devices by JAX's collectives and lax.ppermute only.
A program may use at most 64 MiB of HBM per device.

v0:
```python
import jax
import jax.numpy as jnp
from jax import lax
from jax.sharding import Mesh
from jax.sharding import PartitionSpec as P

ITERS = 2
GRP = ("grp_0", "grp_1")
MEM = ("mem_0", "mem_1")
GRP_MEM = ("grp_0", "grp_1", "mem_0", "mem_1")


def one_axis_at_a_time(x, axes):
    for axis in axes:
        x = lax.psum(x, axis)
    return x


def pack_panels(panels, targets, peers):
    placing = (targets[:, None] == jnp.arange(peers, dtype=jnp.int32)[None, :]).astype(jnp.bfloat16)
    return jnp.einsum("tk,trh->krh", placing, panels, preferred_element_type=jnp.float32).astype(
        jnp.bfloat16
    )


def unpack_panels(received, chosen):
    return jnp.einsum(
        "kt,krh->trh", chosen.astype(jnp.bfloat16), received, preferred_element_type=jnp.float32
    ).astype(jnp.bfloat16)


def cross_groups(panels, group_steps):
    peers = lax.axis_size(GRP)
    own_group = lax.axis_index(GRP)
    outgoing = pack_panels(panels, (own_group + group_steps) % peers, peers)
    received = lax.all_to_all(outgoing, GRP, split_axis=0, concat_axis=0, tiled=True)
    anchors = (
        jnp.arange(peers, dtype=jnp.int32)[:, None] + group_steps[None, :]
    ) % peers == own_group
    return unpack_panels(received, anchors)


def cross_members(panels, member_steps):
    peers = lax.axis_size(MEM)
    own_member = lax.axis_index(MEM)
    outgoing = pack_panels(panels, (own_member + member_steps) % peers, peers)
    received = lax.all_to_all(outgoing, MEM, split_axis=0, concat_axis=0, tiled=True)
    anchors = (
        jnp.arange(peers, dtype=jnp.int32)[:, None] + member_steps[None, :]
    ) % peers == own_member
    return unpack_panels(received, anchors)


def route_panels(panels, group_steps, member_steps):
    moved = cross_groups(panels, group_steps)
    return cross_members(moved, member_steps)


def on_device(v_stack, u_stack, warm_start, observed, owners, tile_ranks):
    group_count = lax.axis_size(GRP)
    member_count = lax.axis_size(MEM)
    slots_held = owners.shape[1]
    stack_width = v_stack.shape[1]
    rank_cap = stack_width // slots_held
    right_count = warm_start.shape[1]
    live_rows = (
        lax.broadcasted_iota(jnp.int32, (slots_held, rank_cap), 1) < tile_ranks[0][:, None]
    ).astype(jnp.float32)
    forward_groups = owners[0] // member_count % group_count
    forward_members = owners[0] % member_count
    backward_groups = (group_count - forward_groups) % group_count
    backward_members = (member_count - forward_members) % member_count

    def forward(field):
        panels = jnp.einsum("bk,bh->kh", v_stack, field, preferred_element_type=jnp.float32)
        panels = (panels.reshape(slots_held, rank_cap, right_count) * live_rows[:, :, None]).astype(
            jnp.bfloat16
        )
        arrived = route_panels(panels, forward_groups, forward_members)
        return jnp.dot(
            u_stack, arrived.reshape(stack_width, right_count), preferred_element_type=jnp.float32
        )

    def adjoint(field):
        panels = jnp.einsum("bk,bh->kh", u_stack, field, preferred_element_type=jnp.float32)
        panels = panels.reshape(slots_held, rank_cap, right_count).astype(jnp.bfloat16)
        returned = route_panels(panels, backward_groups, backward_members)
        masked = (returned * live_rows[:, :, None]).astype(jnp.bfloat16)
        return jnp.dot(
            v_stack, masked.reshape(stack_width, right_count), preferred_element_type=jnp.float32
        )

    model = warm_start.astype(jnp.float32)
    residual = forward(warm_start) - observed.astype(jnp.float32)
    entries = float(warm_start.shape[0] * right_count * group_count * member_count)

    def iterate(index, carry):
        model, residual = carry
        spread = one_axis_at_a_time(jnp.sum(jnp.abs(residual)), GRP_MEM)
        huber_scale = 1.345 * spread / entries + 1e-06
        weights = huber_scale / jnp.maximum(jnp.abs(residual), huber_scale)
        weighted = (weights * residual).astype(jnp.bfloat16)
        gradient = adjoint(weighted)
        grad_sum = one_axis_at_a_time(jnp.sum(gradient * gradient), GRP_MEM)
        image_dir = forward(gradient.astype(jnp.bfloat16))
        curve_sum = one_axis_at_a_time(jnp.sum(weights * image_dir * image_dir), GRP_MEM)
        step_size = grad_sum / (curve_sum + 1e-06)
        return (model - step_size * gradient, residual - step_size * image_dir)

    model, residual = lax.fori_loop(0, ITERS, iterate, (model, residual))
    return (model, residual.astype(jnp.bfloat16))


def solution(mesh):
    finer = Mesh(mesh.devices.reshape(8, 2, 4, 8), ("grp_0", "grp_1", "mem_0", "mem_1"))
    placed = (
        P(GRP_MEM, None),
        P(GRP_MEM, None),
        P(GRP_MEM, None),
        P(GRP_MEM, None),
        P(),
        P(GRP_MEM, None),
    )
    return jax.shard_map(
        on_device,
        mesh=finer,
        in_specs=placed,
        out_specs=(P(GRP_MEM, None), P(GRP_MEM, None)),
        check_vma=False,
    )
```

profile of v0, /device:TPU:1, one launch (start us, length us, event | category | flops | bytes accessed | tf_op | source)
XLA Modules:
  0.0 709.5 jit_solution(6937026796179106969)
XLA Ops:
  6.2 10.3 %all-to-all-start.4 = ((bf16[16,128,256]{2,1,0:T(8,128)(2,1)}), bf16[16,128,256]{2,1,0:T(8,128)(2,1)S(1)}, u32[]{:S(2)}, u32[]{:S(2)}) async-start(bf16[16,128,256]{2,1,0:T(8,128)(2,1)} %copy.53), calls=%async_computation.4 | async-start | bytes 2097152 | tf_op jit(solution)/shard_map/all_to_all | solution.py:36
  16.5 28.0 %all-to-all-done.4 = bf16[16,128,256]{2,1,0:T(8,128)(2,1)S(1)} async-done(((bf16[16,128,256]{2,1,0:T(8,128)(2,1)}), bf16[16,128,256]{2,1,0:T(8,128)(2,1)S(1)}, u32[]{:S(2)}, u32[]{:S(2)}) %all-to-all-start.4) | async-done | bytes 1048608 | tf_op jit(solution)/shard_map/all_to_all | solution.py:36
  48.3 11.3 %all-to-all-start.5 = ((bf16[32,128,256]{2,1,0:T(8,128)(2,1)}), bf16[32,128,256]{2,1,0:T(8,128)(2,1)S(1)}, u32[]{:S(2)}, u32[]{:S(2)}) async-start(bf16[32,128,256]{2,1,0:T(8,128)(2,1)} %copy.55), calls=%async_computation.5 | async-start | bytes 4194304 | tf_op jit(solution)/shard_map/all_to_all | solution.py:47
  63.0 46.1 %all-to-all-done.5 = bf16[32,128,256]{2,1,0:T(8,128)(2,1)S(1)} async-done(((bf16[32,128,256]{2,1,0:T(8,128)(2,1)}), bf16[32,128,256]{2,1,0:T(8,128)(2,1)S(1)}, u32[]{:S(2)}, u32[]{:S(2)}) %all-to-all-start.5) | async-done | bytes 2097184 | tf_op jit(solution)/shard_map/all_to_all | solution.py:47
  113.2 591.6 %while.16 = (s32[]{:T(128)}, f32[1024,256]{0,1:T(8,128)}, f32[1024,256]{0,1:T(8,128)}, s32[4]{0:T(128)S(1)}, s32[4]{0:T(128)S(1)}, /*index=5*/bf16[1024,512]{1,0...) while((s32[]{:T(128)}, f32[1024,256]{0,1:T(8,128)}, ...), condition=%wide.region_16.17_spmd.clone, body=%wide.region_0.16_spmd.clone.sunk | while | flops 1133779456 | bytes 70786008 | solution.py:110
  115.3 11.3 %psum.148 = f32[]{:T(128)} all-reduce(f32[]{:T(128)} %abs_reduce_fusion.2), channel_id=1, replica_groups=mesh['grp_0'=8,'grp_1'=2,'mem_0'=4,'mem_1'=8] {'grp_0'}, use_global_device_ids=true, to_apply=%region_2.2 | all-reduce | flops 1 | bytes 8 | tf_op jit(solution)/shard_map/while/body/eval_jaxpr/psum | solution.py:15
  141.3 13.3 %psum.151 = f32[]{:T(128)} all-reduce(f32[]{:T(128)} %psum.150), channel_id=1, replica_groups=mesh['grp_0'=8,'grp_1'=2,'mem_0'=4,'mem_1'=8] {'mem_1'}, use_global_device_ids=true, to_apply=%region_5.5 | all-reduce | flops 1 | bytes 8 | tf_op jit(solution)/shard_map/while/body/eval_jaxpr/psum | solution.py:15
  159.5 12.1 %all-to-all-start = ((bf16[16,128,256]{2,1,0:T(8,128)(2,1)}), bf16[16,128,256]{2,1,0:T(8,128)(2,1)}, u32[]{:S(2)}, u32[]{:S(2)}) async-start(bf16[16,128,256]{2,1,0:T(8,128)(2,1)} %copy.115), calls=%async_computation | async-start | bytes 2097152 | tf_op jit(solution)/shard_map/while/body/eval_jaxpr/all_to_all | solution.py:36
  171.6 28.1 %all-to-all-done = bf16[16,128,256]{2,1,0:T(8,128)(2,1)} async-done(((bf16[16,128,256]{2,1,0:T(8,128)(2,1)}), bf16[16,128,256]{2,1,0:T(8,128)(2,1)}, u32[]{:S(2)}, u32[]{:S(2)}) %all-to-all-start) | async-done | bytes 1048608 | tf_op jit(solution)/shard_map/while/body/eval_jaxpr/all_to_all | solution.py:36
  210.4 49.4 %all-to-all-done.1 = bf16[32,128,256]{2,1,0:T(8,128)(2,1)S(1)} async-done(((bf16[32,128,256]{2,1,0:T(8,128)(2,1)}), bf16[32,128,256]{2,1,0:T(8,128)(2,1)S(1)}, u32[]{:S(2)}, u32[]{:S(2)}) %all-to-all-start.1) | async-done | bytes 2097184 | tf_op jit(solution)/shard_map/while/body/eval_jaxpr/all_to_all | solution.py:47
  269.7 28.1 %all-to-all-done.2 = bf16[16,128,256]{2,1,0:T(8,128)(2,1)} async-done(((bf16[16,128,256]{2,1,0:T(8,128)(2,1)}), bf16[16,128,256]{2,1,0:T(8,128)(2,1)}, u32[]{:S(2)}, u32[]{:S(2)}) %all-to-all-start.2) | async-done | bytes 1048608 | tf_op jit(solution)/shard_map/while/body/eval_jaxpr/all_to_all | solution.py:36
  309.5 49.5 %all-to-all-done.3 = bf16[32,128,256]{2,1,0:T(8,128)(2,1)S(1)} async-done(((bf16[32,128,256]{2,1,0:T(8,128)(2,1)}), bf16[32,128,256]{2,1,0:T(8,128)(2,1)S(1)}, u32[]{:S(2)}, u32[]{:S(2)}) %all-to-all-start.3) | async-done | bytes 2097184 | tf_op jit(solution)/shard_map/while/body/eval_jaxpr/all_to_all | solution.py:47
  363.0 11.4 %all-reduce.8 = (f32[]{:T(128)}, f32[]{:T(128)}) all-reduce(f32[]{:T(128)} %get-tuple-element.315, f32[]{:T(128)} %get-tuple-element.316), channel_id=1, replica_groups=mesh['grp_0'=8,'grp_1'=2,'mem_0'=4,'mem_1'=8] {'grp_0'}, use_global_device_ids=true, to_apply=%region_7.7 | all-reduce | flops 2 | bytes 16 | tf_op jit(solution)/shard_map/while/body/eval_jaxpr/psum | solution.py:15
  389.0 13.5 %all-reduce.11 = (f32[]{:T(128)}, f32[]{:T(128)}) all-reduce(f32[]{:T(128)} %get-tuple-element.321, f32[]{:T(128)} %get-tuple-element.322), channel_id=1, replica_groups=mesh['grp_0'=8,'grp_1'=2,'mem_0'=4,'mem_1'=8] {'mem_1'}, use_global_device_ids=true, to_apply=%region_10.10 | all-reduce | flops 2 | bytes 16 | tf_op jit(solution)/shard_map/while/body/eval_jaxpr/psum | solution.py:15
  409.2 13.1 %psum.148 = f32[]{:T(128)} all-reduce(f32[]{:T(128)} %abs_reduce_fusion.2), channel_id=1, replica_groups=mesh['grp_0'=8,'grp_1'=2,'mem_0'=4,'mem_1'=8] {'grp_0'}, use_global_device_ids=true, to_apply=%region_2.2 | all-reduce | flops 1 | bytes 8 | tf_op jit(solution)/shard_map/while/body/eval_jaxpr/psum | solution.py:15
  422.3 12.5 %psum.149 = f32[]{:T(128)} all-reduce(f32[]{:T(128)} %psum.148), channel_id=1, replica_groups=mesh['grp_0'=8,'grp_1'=2,'mem_0'=4,'mem_1'=8] {'grp_1'}, use_global_device_ids=true, to_apply=%region_3.3 | all-reduce | flops 1 | bytes 8 | tf_op jit(solution)/shard_map/while/body/eval_jaxpr/psum | solution.py:15
  441.5 11.3 %psum.151 = f32[]{:T(128)} all-reduce(f32[]{:T(128)} %psum.150), channel_id=1, replica_groups=mesh['grp_0'=8,'grp_1'=2,'mem_0'=4,'mem_1'=8] {'mem_1'}, use_global_device_ids=true, to_apply=%region_5.5 | all-reduce | flops 1 | bytes 8 | tf_op jit(solution)/shard_map/while/body/eval_jaxpr/psum | solution.py:15
  457.7 10.9 %all-to-all-start = ((bf16[16,128,256]{2,1,0:T(8,128)(2,1)}), bf16[16,128,256]{2,1,0:T(8,128)(2,1)}, u32[]{:S(2)}, u32[]{:S(2)}) async-start(bf16[16,128,256]{2,1,0:T(8,128)(2,1)} %copy.115), calls=%async_computation | async-start | bytes 2097152 | tf_op jit(solution)/shard_map/while/body/eval_jaxpr/all_to_all | solution.py:36
  468.6 28.1 %all-to-all-done = bf16[16,128,256]{2,1,0:T(8,128)(2,1)} async-done(((bf16[16,128,256]{2,1,0:T(8,128)(2,1)}), bf16[16,128,256]{2,1,0:T(8,128)(2,1)}, u32[]{:S(2)}, u32[]{:S(2)}) %all-to-all-start) | async-done | bytes 1048608 | tf_op jit(solution)/shard_map/while/body/eval_jaxpr/all_to_all | solution.py:36
  508.1 49.4 %all-to-all-done.1 = bf16[32,128,256]{2,1,0:T(8,128)(2,1)S(1)} async-done(((bf16[32,128,256]{2,1,0:T(8,128)(2,1)}), bf16[32,128,256]{2,1,0:T(8,128)(2,1)S(1)}, u32[]{:S(2)}, u32[]{:S(2)}) %all-to-all-start.1) | async-done | bytes 2097184 | tf_op jit(solution)/shard_map/while/body/eval_jaxpr/all_to_all | solution.py:47
  567.4 28.1 %all-to-all-done.2 = bf16[16,128,256]{2,1,0:T(8,128)(2,1)} async-done(((bf16[16,128,256]{2,1,0:T(8,128)(2,1)}), bf16[16,128,256]{2,1,0:T(8,128)(2,1)}, u32[]{:S(2)}, u32[]{:S(2)}) %all-to-all-start.2) | async-done | bytes 1048608 | tf_op jit(solution)/shard_map/while/body/eval_jaxpr/all_to_all | solution.py:36
  607.2 49.5 %all-to-all-done.3 = bf16[32,128,256]{2,1,0:T(8,128)(2,1)S(1)} async-done(((bf16[32,128,256]{2,1,0:T(8,128)(2,1)}), bf16[32,128,256]{2,1,0:T(8,128)(2,1)S(1)}, u32[]{:S(2)}, u32[]{:S(2)}) %all-to-all-start.3) | async-done | bytes 2097184 | tf_op jit(solution)/shard_map/while/body/eval_jaxpr/all_to_all | solution.py:47
  660.7 11.4 %all-reduce.8 = (f32[]{:T(128)}, f32[]{:T(128)}) all-reduce(f32[]{:T(128)} %get-tuple-element.315, f32[]{:T(128)} %get-tuple-element.316), channel_id=1, replica_groups=mesh['grp_0'=8,'grp_1'=2,'mem_0'=4,'mem_1'=8] {'grp_0'}, use_global_device_ids=true, to_apply=%region_7.7 | all-reduce | flops 2 | bytes 16 | tf_op jit(solution)/shard_map/while/body/eval_jaxpr/psum | solution.py:15
  686.7 13.4 %all-reduce.11 = (f32[]{:T(128)}, f32[]{:T(128)}) all-reduce(f32[]{:T(128)} %get-tuple-element.321, f32[]{:T(128)} %get-tuple-element.322), channel_id=1, replica_groups=mesh['grp_0'=8,'grp_1'=2,'mem_0'=4,'mem_1'=8] {'mem_1'}, use_global_device_ids=true, to_apply=%region_10.10 | all-reduce | flops 2 | bytes 16 | tf_op jit(solution)/shard_map/while/body/eval_jaxpr/psum | solution.py:15
  (95 shorter events, 164.7 us)
Async XLA Ops:
  6.2 38.3 %all-to-all-start.4 = ((bf16[16,128,256]{2,1,0:T(8,128)(2,1)}), bf16[16,128,256]{2,1,0:T(8,128)(2,1)S(1)}, u32[]{:S(2)}, u32[]{:S(2)}) async-start(bf16[16,128,256]{2,1,0:T(8,128)(2,1)} %copy.53), calls=%async_computation.4 | async-start | bytes 2097152 | tf_op jit(solution)/shard_map/all_to_all | solution.py:36
  48.3 11.3 %copy-start.3 = (bf16[1024,256]{1,0:T(8,128)(2,1)S(1)}, bf16[1024,256]{1,0:T(8,128)(2,1)}, u32[]{:S(2)}) copy-start(bf16[1024,256]{1,0:T(8,128)(2,1)} %param.10) | copy-start | bytes 1572868
  48.3 60.8 %all-to-all-start.5 = ((bf16[32,128,256]{2,1,0:T(8,128)(2,1)}), bf16[32,128,256]{2,1,0:T(8,128)(2,1)S(1)}, u32[]{:S(2)}, u32[]{:S(2)}) async-start(bf16[32,128,256]{2,1,0:T(8,128)(2,1)} %copy.55), calls=%async_computation.5 | async-start | bytes 4194304 | tf_op jit(solution)/shard_map/all_to_all | solution.py:47
  109.1 1.3 copy-start.2
  110.4 2.8 copy-start
  110.4 2.8 copy-start.4
  159.5 40.2 %all-to-all-start = ((bf16[16,128,256]{2,1,0:T(8,128)(2,1)}), bf16[16,128,256]{2,1,0:T(8,128)(2,1)}, u32[]{:S(2)}, u32[]{:S(2)}) async-start(bf16[16,128,256]{2,1,0:T(8,128)(2,1)} %copy.115), calls=%async_computation | async-start | bytes 2097152 | tf_op jit(solution)/shard_map/while/body/eval_jaxpr/all_to_all | solution.py:36
  204.7 55.0 %all-to-all-start.1 = ((bf16[32,128,256]{2,1,0:T(8,128)(2,1)}), bf16[32,128,256]{2,1,0:T(8,128)(2,1)S(1)}, u32[]{:S(2)}, u32[]{:S(2)}) async-start(bf16[32,128,256]{2,1,0:T(8,128)(2,1)} %copy.116), calls=%async_computation.1 | async-start | bytes 4194304 | tf_op jit(solution)/shard_map/while/body/eval_jaxpr/all_to_all | solution.py:47
  265.1 32.7 %all-to-all-start.2 = ((bf16[16,128,256]{2,1,0:T(8,128)(2,1)}), bf16[16,128,256]{2,1,0:T(8,128)(2,1)}, u32[]{:S(2)}, u32[]{:S(2)}) async-start(bf16[16,128,256]{2,1,0:T(8,128)(2,1)} %copy.119), calls=%async_computation.2 | async-start | bytes 2097152 | tf_op jit(solution)/shard_map/while/body/eval_jaxpr/all_to_all | solution.py:36
  302.8 56.1 %all-to-all-start.3 = ((bf16[32,128,256]{2,1,0:T(8,128)(2,1)}), bf16[32,128,256]{2,1,0:T(8,128)(2,1)S(1)}, u32[]{:S(2)}, u32[]{:S(2)}) async-start(bf16[32,128,256]{2,1,0:T(8,128)(2,1)} %copy.120), calls=%async_computation.3 | async-start | bytes 4194304 | tf_op jit(solution)/shard_map/while/body/eval_jaxpr/all_to_all | solution.py:47
  403.7 3.4 copy-start.1
  457.7 39.0 %all-to-all-start = ((bf16[16,128,256]{2,1,0:T(8,128)(2,1)}), bf16[16,128,256]{2,1,0:T(8,128)(2,1)}, u32[]{:S(2)}, u32[]{:S(2)}) async-start(bf16[16,128,256]{2,1,0:T(8,128)(2,1)} %copy.115), calls=%async_computation | async-start | bytes 2097152 | tf_op jit(solution)/shard_map/while/body/eval_jaxpr/all_to_all | solution.py:36
  501.7 55.8 %all-to-all-start.1 = ((bf16[32,128,256]{2,1,0:T(8,128)(2,1)}), bf16[32,128,256]{2,1,0:T(8,128)(2,1)S(1)}, u32[]{:S(2)}, u32[]{:S(2)}) async-start(bf16[32,128,256]{2,1,0:T(8,128)(2,1)} %copy.116), calls=%async_computation.1 | async-start | bytes 4194304 | tf_op jit(solution)/shard_map/while/body/eval_jaxpr/all_to_all | solution.py:47
  562.9 32.7 %all-to-all-start.2 = ((bf16[16,128,256]{2,1,0:T(8,128)(2,1)}), bf16[16,128,256]{2,1,0:T(8,128)(2,1)}, u32[]{:S(2)}, u32[]{:S(2)}) async-start(bf16[16,128,256]{2,1,0:T(8,128)(2,1)} %copy.119), calls=%async_computation.2 | async-start | bytes 2097152 | tf_op jit(solution)/shard_map/while/body/eval_jaxpr/all_to_all | solution.py:36
  600.6 56.1 %all-to-all-start.3 = ((bf16[32,128,256]{2,1,0:T(8,128)(2,1)}), bf16[32,128,256]{2,1,0:T(8,128)(2,1)S(1)}, u32[]{:S(2)}, u32[]{:S(2)}) async-start(bf16[32,128,256]{2,1,0:T(8,128)(2,1)} %copy.120), calls=%async_computation.3 | async-start | bytes 4194304 | tf_op jit(solution)/shard_map/while/body/eval_jaxpr/all_to_all | solution.py:47
  701.4 3.4 copy-start.1
where the time goes:
time: 716 us; the launch traced here: 710 us
  waiting for transfers between devices  384 us (54%)
  blocking collectives  162 us (23%)
  starting transfers between devices  78.9 us (11%)
  matrix products  38.4 us (5%)
  local copies, waits for them, and re-layouts  27.6 us (4%)
  other arithmetic  13.7 us (2%)
    all_to_all x5, waiting for transfers between devices, cross_members(): lax.all_to_all(outgoing, MEM, split_axis=0, concat_axis=0, tiled=True)  244 us
    psum x16, blocking collectives, one_axis_at_a_time(): x = lax.psum(x, axis)  162 us
    all_to_all x5, waiting for transfers between devices, cross_groups(): lax.all_to_all(outgoing, GRP, split_axis=0, concat_axis=0, tiled=True)  140 us
    all_to_all x5, starting transfers between devices, cross_groups(): lax.all_to_all(outgoing, GRP, split_axis=0, concat_axis=0, tiled=True)  42.4 us
    all_to_all x5, starting transfers between devices, cross_members(): lax.all_to_all(outgoing, MEM, split_axis=0, concat_axis=0, tiled=True)  36.4 us
    convert_element_type x10, local copies, waits for them, and re-layouts, pack_panels(): jnp.einsum('tk,trh->krh', placing, panels, preferred_element_type=jnp.flo...  19.5 us
    dot_general x10, matrix products, pack_panels(): jnp.einsum('tk,trh->krh', placing, panels, preferred_element_type=jnp.flo...  15 us
  transfers between devices with their start and end apart: 10, of which 10 were waited for; matrix products, arithmetic and copies ran while one was open for 0% of the time, Pallas kernels for 0%

commit v1 on v0

v1 whole, which is shorter than its diff:
```python
import jax
import jax.numpy as jnp
from jax import lax
from jax.sharding import PartitionSpec as P

ITERS = 2
ALL = ("grp", "mem")


def total(values):
    k = values.shape[0]
    for axis in ALL:
        n = lax.axis_size(axis)
        spread = jnp.broadcast_to(values[None, :, None], (n, k, 128))
        got = lax.all_to_all(spread, axis, split_axis=0, concat_axis=0, tiled=True)
        values = jnp.sum(got[:, :, 0], axis=0)
    return values


def on_device(v_stack, u_stack, warm_start, observed, owners, tile_ranks):
    group_count = lax.axis_size("grp")
    member_count = lax.axis_size("mem")
    devices = group_count * member_count
    slots = owners.shape[1]
    width = v_stack.shape[1]
    rank_cap = width // slots
    rhs = warm_start.shape[1]
    live = (
        lax.broadcasted_iota(jnp.int32, (slots, rank_cap, 1), 1) < tile_ranks[0][:, None, None]
    ).reshape(width, 1)
    me = lax.axis_index(ALL)
    mine = lax.dynamic_index_in_dim(owners[0], me // (devices // slots), 0, keepdims=False)
    lead = mine // member_count
    shift = mine % member_count
    scatter = (lambda x: lax.all_to_all(x, ALL, split_axis=0, concat_axis=0, tiled=True))

    def route(panels, lead, shift):
        x = scatter(panels.reshape(devices, rhs // 128, 128))
        x = x.reshape(group_count, member_count, rhs // 128, 128)
        x = jnp.roll(x, (lead, shift), axis=(0, 1))
        x = scatter(x.reshape(devices, rhs // 128, 128))
        return x.reshape(width, rhs)

    def forward(field):
        panels = lax.dot_general(
            v_stack, field, (((0,), (0,)), ((), ())), preferred_element_type=jnp.float32
        )
        panels = jnp.where(live, panels, 0.0).astype(jnp.bfloat16)
        arrived = route(panels, lead, shift)
        return jnp.dot(u_stack, arrived, preferred_element_type=jnp.float32)

    def adjoint(field):
        panels = lax.dot_general(
            u_stack, field, (((0,), (0,)), ((), ())), preferred_element_type=jnp.float32
        ).astype(jnp.bfloat16)
        back = route(panels, (group_count - lead) % group_count, (member_count - shift) % member_count)
        back = jnp.where(live, back, jnp.zeros_like(back))
        return jnp.dot(v_stack, back, preferred_element_type=jnp.float32)

    model = warm_start.astype(jnp.float32)
    residual = forward(warm_start) - observed.astype(jnp.float32)
    entries = float(warm_start.shape[0] * rhs * devices)

    def iterate(_, carry):
        model, residual = carry
        spread = total(jnp.sum(jnp.abs(residual))[None])[0]
        scale = 1.345 * spread / entries + 1e-06
        weights = scale / jnp.maximum(jnp.abs(residual), scale)
        weighted = (weights * residual).astype(jnp.bfloat16)
        gradient = adjoint(weighted)
        image = forward(gradient.astype(jnp.bfloat16))
        sums = total(
            jnp.stack([jnp.sum(gradient * gradient), jnp.sum(weights * image * image)])
        )
        step = sums[0] / (sums[1] + 1e-06)
        model = model - step * gradient
        residual = residual - step * image
        return model, residual

    model, residual = lax.fori_loop(0, ITERS, iterate, (model, residual))
    return model, residual.astype(jnp.bfloat16)


def solution(mesh):
    rows = P(ALL, None)
    return jax.shard_map(
        on_device,
        mesh=mesh,
        in_specs=(rows, rows, rows, rows, P(), rows),
        out_specs=(rows, rows),
        check_vma=False,
    )
```

time: 716 us -> 428 us (0.60)
  waiting for transfers between devices: 384 us -> 128 us
  blocking collectives: 162 us -> 122 us
  matrix products: 38.4 us -> 14.4 us
  starting transfers between devices: 78.9 us -> 98.3 us
  loops' own time: 4.01 us -> 19.4 us
    all_to_all x10, waiting for transfers between devices: 384 us -> 128 us  [the longest x8 111 us: on_device(): lax.all_to_all(x, ALL, split_axis=0, concat_axis=0, tiled=True)]
    psum x16 -> x0, blocking collectives: 162 us -> none  [one_axis_at_a_time(): x = lax.psum(x, axis)]
    all_to_all x0 -> x8, blocking collectives: none -> 122 us  [the longest x6 68.3 us: total(): got = lax.all_to_all(spread, axis, split_axis=0, concat_axis=0, tiled=True)]
    dot_general x25 -> x10, matrix products: 38.4 us -> 14.4 us  [the longest x3 8.53 us: forward(): return jnp.dot(u_stack, arrived, preferred_element_type=jnp.float32)]
    convert_element_type x19 -> x0, local copies, waits for them, and re-layouts: 20.2 us -> none  [the longest x10 19.5 us: pack_panels(): jnp.einsum('tk,trh->krh', placing, panels, preferred_element_type=jnp.flo...]
    all_to_all x10, starting transfers between devices: 78.9 us -> 98.3 us  [the longest x8 89.4 us: on_device(): lax.all_to_all(x, ALL, split_axis=0, concat_axis=0, tiled=True)]
    another operation x1, loops' own time: 4.01 us -> 19.4 us  [on_device(): model, residual = lax.fori_loop(0, ITERS, iterate, (model, residual))]
    reshape x0 -> x10, local copies, waits for them, and re-layouts: none -> 7.82 us  [the longest x5 4.36 us: route(): x = scatter(panels.reshape(devices, rhs // 128, 128))]
  transfers between devices with their start and end apart: 10 -> 10, of which waited for: 10 -> 10; matrix products, arithmetic and copies ran while one was open for 0% -> 1% of each run, Pallas kernels for 0% -> 0%
where the time goes in v1:
time: 428 us; the launch traced here: 426 us
  waiting for transfers between devices  128 us (30%)
  blocking collectives  122 us (29%)
  starting transfers between devices  98.3 us (23%)
  local copies, waits for them, and re-layouts  24 us (6%)
  loops' own time  19.4 us (5%)
  other arithmetic  16.7 us (4%)
  matrix products  14.4 us (3%)
    all_to_all x8, waiting for transfers between devices, on_device(): lax.all_to_all(x, ALL, split_axis=0, concat_axis=0, tiled=True)  111 us
    all_to_all x8, starting transfers between devices, on_device(): lax.all_to_all(x, ALL, split_axis=0, concat_axis=0, tiled=True)  89.4 us
    all_to_all x6, blocking collectives, total(): got = lax.all_to_all(spread, axis, split_axis=0, concat_axis=0, tiled=True)  68.3 us
    all_to_all x2, blocking collectives, on_device(): lax.all_to_all(x, ALL, split_axis=0, concat_axis=0, tiled=True)  53.3 us
    another operation x1, loops' own time, on_device(): model, residual = lax.fori_loop(0, ITERS, iterate, (model, residual))  19.4 us
    all_to_all x2, waiting for transfers between devices, total(): got = lax.all_to_all(spread, axis, split_axis=0, concat_axis=0, tiled=True)  17.5 us
    all_to_all x2, starting transfers between devices, total(): got = lax.all_to_all(spread, axis, split_axis=0, concat_axis=0, tiled=True)  8.97 us
  transfers between devices with their start and end apart: 10, of which 10 were waited for; matrix products, arithmetic and copies ran while one was open for 1% of the time, Pallas kernels for 0%

profile of v1, /device:TPU:1, one launch (start us, length us, event | category | flops | bytes accessed | tf_op | source)
XLA Modules:
  0.0 426.1 jit_solution(3423159892188849759)
XLA Ops:
  4.1 22.1 %all-to-all-start.8 = ((bf16[512,2,128]{2,1,0:T(2,128)(2,1)}), bf16[512,2,128]{2,1,0:T(2,128)(2,1)S(1)}, u32[]{:S(2)}, u32[]{:S(2)}) async-start(bf16[512,2,128]{2,1,0:T(2,128)(2,1)} %copy.74), calls=%async_computation.8 | async-start | bytes 524288 | tf_op jit(solution)/shard_map/all_to_all | solution.py:35
  30.1 12.8 %all-to-all-done.8 = bf16[512,2,128]{2,1,0:T(2,128)(2,1)S(1)} async-done(((bf16[512,2,128]{2,1,0:T(2,128)(2,1)}), bf16[512,2,128]{2,1,0:T(2,128)(2,1)S(1)}, u32[]{:S(2)}, u32[]{:S(2)}) %all-to-all-start.8) | async-done | bytes 262176 | tf_op jit(solution)/shard_map/all_to_all | solution.py:35
  44.3 9.4 %all-to-all-start.9 = ((bf16[512,2,128]{2,1,0:T(2,128)(2,1)}), bf16[512,2,128]{2,1,0:T(2,128)(2,1)S(1)}, u32[]{:S(2)}, u32[]{:S(2)}) async-start(bf16[512,2,128]{2,1,0:T(2,128)(2,1)} %copy.76), calls=%async_computation.9 | async-start | bytes 524288 | tf_op jit(solution)/shard_map/all_to_all | solution.py:35
  56.2 14.4 %all-to-all-done.9 = bf16[512,2,128]{2,1,0:T(2,128)(2,1)S(1)} async-done(((bf16[512,2,128]{2,1,0:T(2,128)(2,1)}), bf16[512,2,128]{2,1,0:T(2,128)(2,1)S(1)}, u32[]{:S(2)}, u32[]{:S(2)}) %all-to-all-start.9) | async-done | bytes 262176 | tf_op jit(solution)/shard_map/all_to_all | solution.py:35
  72.6 350.8 %while.16 = (s32[]{:T(128)}, f32[1024,256]{0,1:T(8,128)}, f32[1024,256]{0,1:T(8,128)S(1)}, bf16[1024,512]{1,0:T(8,128)(2,1)}, s32[2]{0:T(128)S(1)}, /*index=5*/b...) while((s32[]{:T(128)}, f32[1024,256]{0,1:T(8,128)}, ...), condition=%wide.region_8.10_spmd.clone, body=%wide.region_0.9_spmd.clone.sunk | while | flops 1080820224 | bytes 31976652 | solution.py:80
  74.3 10.6 %all_to_all.98 = f32[16,1,128]{2,1,0:T(1,128)S(1)} all-to-all(f32[16,1,128]{2,1,0:T(1,128)S(1)} %broadcast_in_dim.133), channel_id=1, replica_groups=mesh['grp'=16,'mem'=32] {'grp'}, dimensions={0} | all-to-all | bytes 16384 | tf_op jit(solution)/shard_map/while/body/eval_jaxpr/all_to_all | solution.py:15
  86.2 13.0 %all_to_all.99 = f32[32,1,128]{2,1,0:T(1,128)S(1)} all-to-all(f32[32,1,128]{2,1,0:T(1,128)S(1)} %broadcast_in_dim.134), channel_id=1, replica_groups=mesh['grp'=16,'mem'=32] {'mem'}, dimensions={0} | all-to-all | bytes 32768 | tf_op jit(solution)/shard_map/while/body/eval_jaxpr/all_to_all | solution.py:15
  101.8 10.3 %all-to-all-start.2 = ((bf16[512,2,128]{2,1,0:T(2,128)(2,1)}), bf16[512,2,128]{2,1,0:T(2,128)(2,1)S(1)}, u32[]{:S(2)}, u32[]{:S(2)}) async-start(bf16[512,2,128]{2,1,0:T(2,128)(2,1)} %copy.95), calls=%async_computation.2 | async-start | bytes 524288 | tf_op jit(solution)/shard_map/while/body/eval_jaxpr/all_to_all | solution.py:35
  116.5 12.5 %all-to-all-done.2 = bf16[512,2,128]{2,1,0:T(2,128)(2,1)S(1)} async-done(((bf16[512,2,128]{2,1,0:T(2,128)(2,1)}), bf16[512,2,128]{2,1,0:T(2,128)(2,1)S(1)}, u32[]{:S(2)}, u32[]{:S(2)}) %all-to-all-start.2) | async-done | bytes 262176 | tf_op jit(solution)/shard_map/while/body/eval_jaxpr/all_to_all | solution.py:35
  130.3 9.4 %all-to-all-start.3 = ((bf16[512,2,128]{2,1,0:T(2,128)(2,1)}), bf16[512,2,128]{2,1,0:T(2,128)(2,1)S(1)}, u32[]{:S(2)}, u32[]{:S(2)}) async-start(bf16[512,2,128]{2,1,0:T(2,128)(2,1)} %copy.97), calls=%async_computation.3 | async-start | bytes 524288 | tf_op jit(solution)/shard_map/while/body/eval_jaxpr/all_to_all | solution.py:35
  139.8 16.8 %all-to-all-done.3 = bf16[512,2,128]{2,1,0:T(2,128)(2,1)S(1)} async-done(((bf16[512,2,128]{2,1,0:T(2,128)(2,1)}), bf16[512,2,128]{2,1,0:T(2,128)(2,1)S(1)}, u32[]{:S(2)}, u32[]{:S(2)}) %all-to-all-start.3) | async-done | bytes 262176 | tf_op jit(solution)/shard_map/while/body/eval_jaxpr/all_to_all | solution.py:35
  159.3 9.4 %all-to-all-start.4 = ((bf16[512,2,128]{2,1,0:T(2,128)(2,1)}), bf16[512,2,128]{2,1,0:T(2,128)(2,1)S(1)}, u32[]{:S(2)}, u32[]{:S(2)}) async-start(bf16[512,2,128]{2,1,0:T(2,128)(2,1)} %copy.99), calls=%async_computation.4 | async-start | bytes 524288 | tf_op jit(solution)/shard_map/while/body/eval_jaxpr/all_to_all | solution.py:35
  173.1 12.5 %all-to-all-done.4 = bf16[512,2,128]{2,1,0:T(2,128)(2,1)S(1)} async-done(((bf16[512,2,128]{2,1,0:T(2,128)(2,1)}), bf16[512,2,128]{2,1,0:T(2,128)(2,1)S(1)}, u32[]{:S(2)}, u32[]{:S(2)}) %all-to-all-start.4) | async-done | bytes 262176 | tf_op jit(solution)/shard_map/while/body/eval_jaxpr/all_to_all | solution.py:35
  186.2 26.7 %all_to_all.100 = bf16[512,2,128]{2,1,0:T(2,128)(2,1)S(1)} all-to-all(bf16[512,2,128]{2,1,0:T(2,128)(2,1)S(1)} %copy.101), channel_id=1, replica_groups=mesh['grp'=16,'mem'=32] {'grp','mem'}, dimensions={0} | all-to-all | bytes 524288 | tf_op jit(solution)/shard_map/while/body/eval_jaxpr/all_to_all | solution.py:35
  218.5 10.9 %all_to_all.101 = f32[16,2,128]{2,1,0:T(2,128)S(1)} all-to-all(f32[16,2,128]{2,1,0:T(2,128)S(1)} %broadcast_in_dim.135), channel_id=1, replica_groups=mesh['grp'=16,'mem'=32] {'grp'}, dimensions={0} | all-to-all | bytes 32768 | tf_op jit(solution)/shard_map/while/body/eval_jaxpr/all_to_all | solution.py:15
  250.1 11.3 %all_to_all.98 = f32[16,1,128]{2,1,0:T(1,128)S(1)} all-to-all(f32[16,1,128]{2,1,0:T(1,128)S(1)} %broadcast_in_dim.133), channel_id=1, replica_groups=mesh['grp'=16,'mem'=32] {'grp'}, dimensions={0} | all-to-all | bytes 16384 | tf_op jit(solution)/shard_map/while/body/eval_jaxpr/all_to_all | solution.py:15
  262.6 11.6 %all_to_all.99 = f32[32,1,128]{2,1,0:T(1,128)S(1)} all-to-all(f32[32,1,128]{2,1,0:T(1,128)S(1)} %broadcast_in_dim.134), channel_id=1, replica_groups=mesh['grp'=16,'mem'=32] {'mem'}, dimensions={0} | all-to-all | bytes 32768 | tf_op jit(solution)/shard_map/while/body/eval_jaxpr/all_to_all | solution.py:15
  276.9 10.0 %all-to-all-start.2 = ((bf16[512,2,128]{2,1,0:T(2,128)(2,1)}), bf16[512,2,128]{2,1,0:T(2,128)(2,1)S(1)}, u32[]{:S(2)}, u32[]{:S(2)}) async-start(bf16[512,2,128]{2,1,0:T(2,128)(2,1)} %copy.95), calls=%async_computation.2 | async-start | bytes 524288 | tf_op jit(solution)/shard_map/while/body/eval_jaxpr/all_to_all | solution.py:35
  291.3 12.5 %all-to-all-done.2 = bf16[512,2,128]{2,1,0:T(2,128)(2,1)S(1)} async-done(((bf16[512,2,128]{2,1,0:T(2,128)(2,1)}), bf16[512,2,128]{2,1,0:T(2,128)(2,1)S(1)}, u32[]{:S(2)}, u32[]{:S(2)}) %all-to-all-start.2) | async-done | bytes 262176 | tf_op jit(solution)/shard_map/while/body/eval_jaxpr/all_to_all | solution.py:35
  305.2 9.4 %all-to-all-start.3 = ((bf16[512,2,128]{2,1,0:T(2,128)(2,1)}), bf16[512,2,128]{2,1,0:T(2,128)(2,1)S(1)}, u32[]{:S(2)}, u32[]{:S(2)}) async-start(bf16[512,2,128]{2,1,0:T(2,128)(2,1)} %copy.97), calls=%async_computation.3 | async-start | bytes 524288 | tf_op jit(solution)/shard_map/while/body/eval_jaxpr/all_to_all | solution.py:35
  314.6 16.8 %all-to-all-done.3 = bf16[512,2,128]{2,1,0:T(2,128)(2,1)S(1)} async-done(((bf16[512,2,128]{2,1,0:T(2,128)(2,1)}), bf16[512,2,128]{2,1,0:T(2,128)(2,1)S(1)}, u32[]{:S(2)}, u32[]{:S(2)}) %all-to-all-start.3) | async-done | bytes 262176 | tf_op jit(solution)/shard_map/while/body/eval_jaxpr/all_to_all | solution.py:35
  347.9 12.5 %all-to-all-done.4 = bf16[512,2,128]{2,1,0:T(2,128)(2,1)S(1)} async-done(((bf16[512,2,128]{2,1,0:T(2,128)(2,1)}), bf16[512,2,128]{2,1,0:T(2,128)(2,1)S(1)}, u32[]{:S(2)}, u32[]{:S(2)}) %all-to-all-start.4) | async-done | bytes 262176 | tf_op jit(solution)/shard_map/while/body/eval_jaxpr/all_to_all | solution.py:35
  361.0 26.7 %all_to_all.100 = bf16[512,2,128]{2,1,0:T(2,128)(2,1)S(1)} all-to-all(bf16[512,2,128]{2,1,0:T(2,128)(2,1)S(1)} %copy.101), channel_id=1, replica_groups=mesh['grp'=16,'mem'=32] {'grp','mem'}, dimensions={0} | all-to-all | bytes 524288 | tf_op jit(solution)/shard_map/while/body/eval_jaxpr/all_to_all | solution.py:35
  393.3 10.9 %all_to_all.101 = f32[16,2,128]{2,1,0:T(2,128)S(1)} all-to-all(f32[16,2,128]{2,1,0:T(2,128)S(1)} %broadcast_in_dim.135), channel_id=1, replica_groups=mesh['grp'=16,'mem'=32] {'grp'}, dimensions={0} | all-to-all | bytes 32768 | tf_op jit(solution)/shard_map/while/body/eval_jaxpr/all_to_all | solution.py:15
  (101 shorter events, 91.0 us)
Async XLA Ops:
  0.6 0.7 copy-start.5
  4.1 38.9 %all-to-all-start.8 = ((bf16[512,2,128]{2,1,0:T(2,128)(2,1)}), bf16[512,2,128]{2,1,0:T(2,128)(2,1)S(1)}, u32[]{:S(2)}, u32[]{:S(2)}) async-start(bf16[512,2,128]{2,1,0:T(2,128)(2,1)} %copy.74), calls=%async_computation.8 | async-start | bytes 524288 | tf_op jit(solution)/shard_map/all_to_all | solution.py:35
  26.3 0.7 slice-start
  43.4 10.4 %copy-start.3 = (bf16[1024,256]{1,0:T(8,128)(2,1)S(1)}, bf16[1024,256]{1,0:T(8,128)(2,1)}, u32[]{:S(2)}) copy-start(bf16[1024,256]{1,0:T(8,128)(2,1)} %param.12) | copy-start | bytes 1572868
  44.3 26.2 %all-to-all-start.9 = ((bf16[512,2,128]{2,1,0:T(2,128)(2,1)}), bf16[512,2,128]{2,1,0:T(2,128)(2,1)S(1)}, u32[]{:S(2)}, u32[]{:S(2)}) async-start(bf16[512,2,128]{2,1,0:T(2,128)(2,1)} %copy.76), calls=%async_computation.9 | async-start | bytes 524288 | tf_op jit(solution)/shard_map/all_to_all | solution.py:35
  53.8 1.0 copy-start.4
  70.8 1.8 copy-start
  72.8 27.7 %copy-start.2 = (bf16[1024,512]{1,0:T(8,128)(2,1)S(1)}, bf16[1024,512]{1,0:T(8,128)(2,1)}, u32[]{:S(2)}) copy-start(bf16[1024,512]{1,0:T(8,128)(2,1)} %get-tuple-element.363) | copy-start | bytes 3145732 | tf_op jit(solution)/shard_map/while
  101.8 27.2 %all-to-all-start.2 = ((bf16[512,2,128]{2,1,0:T(2,128)(2,1)}), bf16[512,2,128]{2,1,0:T(2,128)(2,1)S(1)}, u32[]{:S(2)}, u32[]{:S(2)}) async-start(bf16[512,2,128]{2,1,0:T(2,128)(2,1)} %copy.95), calls=%async_computation.2 | async-start | bytes 524288 | tf_op jit(solution)/shard_map/while/body/eval_jaxpr/all_to_all | solution.py:35
  130.3 26.2 %all-to-all-start.3 = ((bf16[512,2,128]{2,1,0:T(2,128)(2,1)}), bf16[512,2,128]{2,1,0:T(2,128)(2,1)S(1)}, u32[]{:S(2)}, u32[]{:S(2)}) async-start(bf16[512,2,128]{2,1,0:T(2,128)(2,1)} %copy.97), calls=%async_computation.3 | async-start | bytes 524288 | tf_op jit(solution)/shard_map/while/body/eval_jaxpr/all_to_all | solution.py:35
  159.3 26.2 %all-to-all-start.4 = ((bf16[512,2,128]{2,1,0:T(2,128)(2,1)}), bf16[512,2,128]{2,1,0:T(2,128)(2,1)S(1)}, u32[]{:S(2)}, u32[]{:S(2)}) async-start(bf16[512,2,128]{2,1,0:T(2,128)(2,1)} %copy.99), calls=%async_computation.4 | async-start | bytes 524288 | tf_op jit(solution)/shard_map/while/body/eval_jaxpr/all_to_all | solution.py:35
  230.2 13.3 %all-to-all-start.7 = ((f32[32,2,128]{2,1,0:T(2,128)}), f32[32,2,128]{2,1,0:T(2,128)S(1)}, u32[]{:S(2)}, u32[]{:S(2)}) async-start(f32[32,2,128]{2,1,0:T(2,128)} %broadcast_in_dim.136), calls=%async_computation.7 | async-start | bytes 65536 | tf_op jit(solution)/shard_map/while/body/eval_jaxpr/all_to_all | solution.py:15
  248.6 27.0 %copy-start.2 = (bf16[1024,512]{1,0:T(8,128)(2,1)S(1)}, bf16[1024,512]{1,0:T(8,128)(2,1)}, u32[]{:S(2)}) copy-start(bf16[1024,512]{1,0:T(8,128)(2,1)} %get-tuple-element.363) | copy-start | bytes 3145732 | tf_op jit(solution)/shard_map/while
  276.9 26.9 %all-to-all-start.2 = ((bf16[512,2,128]{2,1,0:T(2,128)(2,1)}), bf16[512,2,128]{2,1,0:T(2,128)(2,1)S(1)}, u32[]{:S(2)}, u32[]{:S(2)}) async-start(bf16[512,2,128]{2,1,0:T(2,128)(2,1)} %copy.95), calls=%async_computation.2 | async-start | bytes 524288 | tf_op jit(solution)/shard_map/while/body/eval_jaxpr/all_to_all | solution.py:35
  305.2 26.2 %all-to-all-start.3 = ((bf16[512,2,128]{2,1,0:T(2,128)(2,1)}), bf16[512,2,128]{2,1,0:T(2,128)(2,1)S(1)}, u32[]{:S(2)}, u32[]{:S(2)}) async-start(bf16[512,2,128]{2,1,0:T(2,128)(2,1)} %copy.97), calls=%async_computation.3 | async-start | bytes 524288 | tf_op jit(solution)/shard_map/while/body/eval_jaxpr/all_to_all | solution.py:35
  334.1 26.2 %all-to-all-start.4 = ((bf16[512,2,128]{2,1,0:T(2,128)(2,1)}), bf16[512,2,128]{2,1,0:T(2,128)(2,1)S(1)}, u32[]{:S(2)}, u32[]{:S(2)}) async-start(bf16[512,2,128]{2,1,0:T(2,128)(2,1)} %copy.99), calls=%async_computation.4 | async-start | bytes 524288 | tf_op jit(solution)/shard_map/while/body/eval_jaxpr/all_to_all | solution.py:35
  405.1 13.3 %all-to-all-start.7 = ((f32[32,2,128]{2,1,0:T(2,128)}), f32[32,2,128]{2,1,0:T(2,128)S(1)}, u32[]{:S(2)}, u32[]{:S(2)}) async-start(f32[32,2,128]{2,1,0:T(2,128)} %broadcast_in_dim.136), calls=%async_computation.7 | async-start | bytes 65536 | tf_op jit(solution)/shard_map/while/body/eval_jaxpr/all_to_all | solution.py:15
  423.4 1.4 copy-start.1
